TPU v7x, 32 devices: a whole 2x2x4 slice. The times are simulated.
32 devices in a mesh: groups: 2 (over y), ep: 16 (over z, x, core).
Axes of the slice: x: 2, y: 2, z: 4, core: 2. Of those that a mesh axis runs over, the one named last changes fastest.
Arguments:
- tokens: bfloat16 [128, 7168], P(('groups', 'ep')), parts along dimension 0, may hold values from -6 to 6
- routes: int32 [128, 8], P(('groups', 'ep')), parts along dimension 0, may hold values from 0 to 15, as said below
- gates: float32 [128, 8], P(('groups', 'ep')), parts along dimension 0, may hold values from 0.05 to 0.6
- gate_weight: bfloat16 [7168, 32768], P(None, 'ep'), may hold values from -0.0625 to 0.0625
- up_weight: bfloat16 [7168, 32768], P(None, 'ep'), may hold values from -0.0625 to 0.0625
- down_weight: bfloat16 [32768, 7168], P('ep'), may hold values from -0.125 to 0.125
Outputs:
- mixed: bfloat16 [128, 7168], P(('groups', 'ep')), parts along dimension 0
There are 2 independent parts, one for each index of `groups`. A program takes and returns all parts, laid end to end along the dimension named above; an argument that names none is the same for every part. Nothing has to cross between parts.
Inputs may be any that keep to these rules, and one draw needn't show every extreme that they name: `routes`: each token names 8 different experts. Among the 4 tokens of one device no expert is named by more than 3 of them, and in every draw one expert is named by exactly 3 tokens of every device.
All inputs are finite; a program needn't handle non-finite values.
Results may differ from a plain program's by a relative error of at most 0.0085.
Values may be sent and summed in bfloat16 or wider, within the bound.
A program may use at most 128 MiB of HBM per device.

v0:
```python
import jax
import jax.numpy as jnp
from jax import lax
from jax.sharding import PartitionSpec as P

EXPERTS = 16
CAP = 3


def expert_forward(block_in, gate_weight, up_weight, down_weight):
    senders, slot_count, model_width = block_in.shape
    flat_rows = block_in.reshape(senders * slot_count, model_width)
    gate_act = jnp.dot(flat_rows, gate_weight, preferred_element_type=jnp.float32)
    up_act = jnp.dot(flat_rows, up_weight, preferred_element_type=jnp.float32)
    hidden = (jax.nn.silu(gate_act) * up_act).astype(jnp.bfloat16)
    result = jnp.dot(hidden, down_weight, preferred_element_type=jnp.float32)
    return result.reshape(senders, slot_count, model_width)


def shards(tokens, routes, gates, gate_weight, up_weight, down_weight):
    tok_rows, model_width = tokens.shape
    devices_ep = lax.axis_size("ep")
    split_count = devices_ep // EXPERTS
    expert_ids = jnp.arange(EXPERTS, dtype=jnp.int32)
    member = routes[:, :, None] == expert_ids[None, None, :]
    chosen = jnp.any(member, axis=1).astype(jnp.int32)
    gate_share = jnp.sum(jnp.where(member, gates[:, :, None], 0.0), axis=1)
    slot_place = jnp.cumsum(chosen, axis=0) - chosen
    slot_ids = jnp.arange(CAP, dtype=jnp.int32)
    slot_pick = (chosen[:, :, None] == 1) & (slot_place[:, :, None] == slot_ids[None, None, :])
    selector = jnp.transpose(slot_pick, (1, 2, 0)).astype(jnp.bfloat16)
    mix_weight = jnp.where(slot_pick, gate_share[:, :, None], 0.0)
    packed = jnp.einsum("ect,td->ecd", selector, tokens, preferred_element_type=jnp.float32).astype(
        jnp.bfloat16
    )
    outgoing = jnp.broadcast_to(packed[:, None], (EXPERTS, split_count, CAP, model_width)).reshape(
        devices_ep, CAP, model_width
    )
    partial_value = expert_forward(
        lax.all_to_all(outgoing, "ep", split_axis=0, concat_axis=0, tiled=True),
        gate_weight,
        up_weight,
        down_weight,
    )
    returned = lax.all_to_all(partial_value, "ep", split_axis=0, concat_axis=0, tiled=True)
    summed = returned.reshape(EXPERTS, split_count, CAP, model_width).sum(axis=1)
    mixed = jnp.einsum("tec,ecd->td", mix_weight, summed, precision=lax.Precision.HIGHEST)
    return mixed.astype(jnp.bfloat16)


def solution(mesh):
    placed = (
        P(("groups", "ep"), None),
        P(("groups", "ep"), None),
        P(("groups", "ep"), None),
        P(None, "ep"),
        P(None, "ep"),
        P("ep", None),
    )
    return jax.shard_map(
        shards, mesh=mesh, in_specs=placed, out_specs=P(("groups", "ep"), None), check_vma=False
    )
```

profile of v0, /device:TPU:15, one launch (start us, length us, event | category | flops | bytes accessed | tf_op | source)
XLA Modules:
  0.0 114.1 jit_solution(17393039308408811121)
XLA Ops:
  0.0 0.0 copy-start
  0.0 0.8 fusion.11
  0.8 0.0 copy-done
  0.8 0.4 convolution_convert_fusion
  1.3 0.6 copy.12
  1.9 28.3 %all_to_all.10 = bf16[16,3,7168]{2,1,0:T(4,128)(2,1)S(1)} all-to-all(bf16[16,3,7168]{2,1,0:T(4,128)(2,1)S(1)} %copy.12), channel_id=1, replica_groups=mesh['groups'=2,'ep'=16] {'ep'}, dimensions={0} | all-to-all | bytes 1376256 | tf_op jit(solution)/shard_map/all_to_all | solution.py:40
  30.2 0.6 reshape.28
  30.8 12.0 %fusion.26 = f32[48,2048]{1,0:T(8,128)S(1)} fusion(bf16[48,7168]{1,0:T(8,128)(2,1)S(1)} %reshape.28, bf16[7168,2048]{1,0:T(8,128)(2,1)} %param.9), kind=kOutput, calls=%fused_computation.33 | convolution fusion | flops 1409286144 | bytes 30441472 | tf_op jit(solution)/shard_map/dot_general | solution.py:13
  42.9 0.0 copy-start.1
  42.9 0.0 copy-start.2
  42.9 20.8 %fusion.2 = f32[48,7168]{1,0:T(8,128)S(1)} fusion(bf16[2048,7168]{1,0:T(8,128)(2,1)} %param.11, bf16[48,7168]{1,0:T(8,128)(2,1)S(1)} %reshape.28, bf16[7168,2048]{1,0:T(8,128)(2,1)} %param.10, f32[48,2048]{1,0:T(8,128)S(1)} %fusion.26), kind=kOutput, calls=%fused_computation.5 | convolution fusion | flops 2819162112 | bytes 61177856 | tf_op jit(solution)/shard_map/dot_general | solution.py:16
  63.7 1.6 %reshape.29 = f32[16,3,7168]{2,1,0:T(4,128)} reshape(f32[48,7168]{1,0:T(8,128)S(1)} %fusion.2) | data formatting | bytes 2752512 | tf_op jit(solution)/shard_map/reshape | solution.py:17
  65.3 4.9 %all-to-all-start.1 = ((f32[16,3,7168]{2,1,0:T(4,128)}), f32[16,3,7168]{2,1,0:T(4,128)S(1)}, u32[]{:S(2)}, u32[]{:S(2)}) async-start(f32[16,3,7168]{2,1,0:T(4,128)} %reshape.29), calls=%async_computation.1 | async-start | bytes 3670016 | tf_op jit(solution)/shard_map/all_to_all | solution.py:45
  70.2 0.0 copy-done.1
  70.2 0.0 copy-done.2
  70.2 0.1 select_reduce_fusion
  70.3 41.7 %all-to-all-done.1 = f32[16,3,7168]{2,1,0:T(4,128)S(1)} async-done(((f32[16,3,7168]{2,1,0:T(4,128)}), f32[16,3,7168]{2,1,0:T(4,128)S(1)}, u32[]{:S(2)}, u32[]{:S(2)}) %all-to-all-start.1) | async-done | bytes 1376288 | tf_op jit(solution)/shard_map/all_to_all | solution.py:45
  112.0 2.1 %fusion = bf16[4,7168]{1,0:T(4,128)(2,1)} fusion(f32[16,3,7168]{2,1,0:T(4,128)S(1)} %all-to-all-done.1, f32[4,16]{1,0:T(4,128)S(1)} %select_reduce_fusion, s32[4,16]{1,0:T(4,128)S(1)} %convert_subtract_fusion, pred[4,16]{1,0:T(4,128)(4,1)S(1)} %get-tuple-element.5), kind=kOutput, calls=%fused_computation.2 | convolution fusion | flops 16544320 | bytes 1434176 | tf_op jit(solution)/shard_map/tec,ecd->td/dot_general | solution.py:47
  (3 shorter events, 0.1 us)
Async XLA Ops:
  0.0 0.8 copy-start
  42.9 27.3 %copy-start.1 = (s32[4,8]{1,0:T(4,128)S(1)}, s32[4,8]{1,0:T(4,128)}, u32[]{:S(2)}) copy-start(s32[4,8]{1,0:T(4,128)} %param.7) | copy-start | bytes 388
  42.9 27.3 %copy-start.2 = (f32[4,8]{1,0:T(4,128)S(1)}, f32[4,8]{1,0:T(4,128)}, u32[]{:S(2)}) copy-start(f32[4,8]{1,0:T(4,128)} %param.8) | copy-start | bytes 388
  65.3 46.7 %all-to-all-start.1 = ((f32[16,3,7168]{2,1,0:T(4,128)}), f32[16,3,7168]{2,1,0:T(4,128)S(1)}, u32[]{:S(2)}, u32[]{:S(2)}) async-start(f32[16,3,7168]{2,1,0:T(4,128)} %reshape.29), calls=%async_computation.1 | async-start | bytes 3670016 | tf_op jit(solution)/shard_map/all_to_all | solution.py:45
where the time goes:
time: 114 us
  waiting for transfers between devices  41.7 us (37%)
  matrix products  35.4 us (31%)
  blocking collectives  28.3 us (25%)
  starting transfers between devices  4.91 us (4%)
  local copies, waits for them, and re-layouts  2.81 us (2%)
    all_to_all x1, waiting for transfers between devices, shards(): lax.all_to_all(partial_value, 'ep', split_axis=0, concat_axis=0, tiled=True)  41.7 us
    all_to_all x1, blocking collectives, shards(): lax.all_to_all(outgoing, 'ep', split_axis=0, concat_axis=0, tiled=True)  28.3 us
    dot_general x1, matrix products, expert_forward(): result = jnp.dot(hidden, down_weight, preferred_element_type=jnp.float32)  20.8 us
    dot_general x1, matrix products, expert_forward(): jnp.dot(flat_rows, gate_weight, preferred_element_type=jnp.float32)  12 us
    all_to_all x1, starting transfers between devices, shards(): lax.all_to_all(partial_value, 'ep', split_axis=0, concat_axis=0, tiled=True)  4.91 us
  transfers between devices with their start and end apart: 1, of which 1 were waited for; matrix products, arithmetic and copies ran while one was open for 0% of the time, Pallas kernels for 0%

commit v1 on v0

v1 whole, which is shorter than its diff:
```python
import functools

import jax
import jax.numpy as jnp
from jax import lax
from jax.experimental import pallas as pl
from jax.experimental.pallas import tpu as pltpu
from jax.sharding import PartitionSpec as P

EXPERTS = 16
SLOTS = 3
AUX = 128


def piece(total, want):
    size = want
    while total % size:
        size //= 2
    return size


def kernel(
    devices, kc, nc, tile,
    tokens, routes, gates, wg, wu, wd, out,
    ring_g, ring_u, down, rx, ax, xf, xb, acc_g, acc_u, hid, share, mine, theirs, sbuf, rbuf,
    tok_sem, g_sem, u_sem, d_sem,
    tx_send, tx_recv, re_send, re_recv, ob_send, ob_recv, rt_send, rt_recv, ax_send, ax_recv,
):
    rows, width = tokens.shape
    hidden = wg.shape[1]
    chips = devices // 2
    units, outs = width // kc, width // nc
    me = lax.axis_index("ep")
    chip, core = me // 2, me % 2
    other = 1 - core
    peer = chip * 2 + other
    mates = chips * rows

    def remote(src, dst, send, recv, dev):
        return pltpu.make_async_remote_copy(
            src_ref=src, dst_ref=dst, send_sem=send, recv_sem=recv,
            device_id={"ep": dev}, device_id_type=pl.DeviceIdType.MESH,
        )

    def load_tokens(j):
        return pltpu.make_async_copy(
            tokens.at[:, pl.ds(j * kc, kc)], rx.at[j, core, chip], tok_sem.at[j]
        )

    def load_g(j):
        s = j % SLOTS
        return pltpu.make_async_copy(wg.at[pl.ds(j * kc, kc), :], ring_g.at[s], g_sem.at[s])

    def load_u(j):
        s = j % SLOTS
        return pltpu.make_async_copy(wu.at[pl.ds(j * kc, kc), :], ring_u.at[s], u_sem.at[s])

    def load_d(c):
        return pltpu.make_async_copy(wd.at[:, pl.ds(c * nc, nc)], down.at[c], d_sem.at[c])

    for j in range(units):
        load_tokens(j).start()
    for j in range(min(SLOTS, units)):
        load_g(j).start()
        load_u(j).start()

    barrier = pltpu.get_barrier_semaphore()
    pl.semaphore_signal(barrier, inc=1, device_id={"ep": peer}, device_id_type=pl.DeviceIdType.MESH)

    @pl.loop(1, chips)
    def _(i):
        to = lax.rem(chip + i, chips) * 2 + core
        pl.semaphore_signal(barrier, inc=1, device_id={"ep": to}, device_id_type=pl.DeviceIdType.MESH)

    lane = lax.broadcasted_iota(jnp.int32, (rows, AUX), 1)
    name = jnp.where(lane < EXPERTS, lane, lane - EXPERTS)
    weight = jnp.zeros((rows, AUX), jnp.float32)
    for k in range(routes.shape[1]):
        weight = weight + jnp.where(routes[:, k : k + 1] == name, gates[:, k : k + 1], 0.0)
    high = weight.astype(jnp.bfloat16).astype(jnp.float32)
    ax[core, chip] = jnp.where(
        lane < EXPERTS, high, jnp.where(lane < 2 * EXPERTS, weight - high, 0.0)
    ).astype(jnp.bfloat16)

    pl.semaphore_wait(barrier, chips)

    for j in range(units):
        load_tokens(j).wait()

        @pl.loop(1, chips)
        def _(i):
            to = lax.rem(chip + i, chips) * 2 + core
            remote(rx.at[j, core, chip], rx.at[j, core, chip], tx_send.at[j], tx_recv.at[j], to).start()

    @pl.loop(1, chips)
    def _(i):
        to = lax.rem(chip + i, chips) * 2 + core
        remote(ax.at[core, chip], ax.at[core, chip], ax_send.at[0], ax_recv.at[0], to).start()

    def many(ref, sem):
        return pltpu.make_async_copy(ref, ref, sem)

    def relay(j):
        return remote(rx.at[j, core], rx.at[j, core], re_send.at[j], re_recv.at[j], peer)

    relay_aux = remote(ax.at[core], ax.at[core], ax_send.at[1], ax_recv.at[1], peer)

    def forward(j):
        many(rx.at[j, 0, pl.ds(0, chips - 1)], tx_recv.at[j]).wait()
        relay(j).start()

    forward(0)
    for c in range(min(1, outs)):
        load_d(c).start()
    issued = 1
    for j in range(units):
        if j + 1 < units:
            forward(j + 1)
        else:
            many(ax.at[0, pl.ds(0, chips - 1)], ax_recv.at[0]).wait()
            relay_aux.start()
        relay(j).wait_recv()
        for half in range(2):
            @pl.loop(0, chips // 2)
            def _(b):
                pair = jnp.concatenate(
                    [rx[j, half, 2 * b].astype(jnp.float32), rx[j, half, 2 * b + 1].astype(jnp.float32)], axis=0
                )
                at = pl.multiple_of(half * mates + b * 2 * rows, 2 * rows)
                xf[pl.ds(at, 2 * rows), :] = pair
        xb[...] = xf[...].astype(jnp.bfloat16)
        load_g(j).wait()
        load_u(j).wait()
        s = j % SLOTS

        @pl.loop(0, hidden // tile)
        def _(n):
            cols = pl.ds(pl.multiple_of(n * tile, tile), tile)
            pg = jnp.dot(xb[...], ring_g[s, :, cols], preferred_element_type=jnp.float32)
            pu = jnp.dot(xb[...], ring_u[s, :, cols], preferred_element_type=jnp.float32)
            if j == 0:
                acc_g[:, cols] = pg
                acc_u[:, cols] = pu
            elif j < units - 1:
                acc_g[:, cols] += pg
                acc_u[:, cols] += pu
            else:
                g = acc_g[:, cols] + pg
                u = acc_u[:, cols] + pu
                hid[:, cols] = (g / (1.0 + jnp.exp(-g)) * u).astype(jnp.bfloat16)

        if j + SLOTS < units:
            load_g(j + SLOTS).start()
            load_u(j + SLOTS).start()
        goal = outs if j + SLOTS + 1 >= units else min(outs, issued + 1)
        while issued < goal:
            load_d(issued).start()
            issued += 1
    while issued < outs:
        load_d(issued).start()
        issued += 1

    relay_aux.wait_recv()
    expert = me // (devices // EXPERTS)
    spot = lax.broadcasted_iota(jnp.int32, (2 * rows, AUX), 1)
    hot = (spot == expert) | (spot == expert + EXPERTS)
    for half in range(2):
        @pl.loop(0, chips // 2)
        def _(b):
            pair = jnp.concatenate(
                [ax[half, 2 * b].astype(jnp.float32), ax[half, 2 * b + 1].astype(jnp.float32)], axis=0
            )
            at = pl.multiple_of(half * mates + b * 2 * rows, 2 * rows)
            total = jnp.sum(jnp.where(hot, pair, 0.0), axis=1, keepdims=True)
            share[pl.ds(at, 2 * rows), :] = jnp.broadcast_to(total, (2 * rows, AUX))

    def swap(c):
        return remote(mine.at[c, other], theirs.at[c], ob_send.at[c], ob_recv.at[c], peer)

    def give(c):
        swap(c).wait_recv()

        @pl.loop(0, chips // 2)
        def _(b):
            at = pl.multiple_of(b * 2 * rows, 2 * rows)
            both = mine[c, core, pl.ds(at, 2 * rows), :] + theirs[c, pl.ds(at, 2 * rows), :]
            sbuf[c, 2 * b] = both[:rows].astype(jnp.bfloat16)
            sbuf[c, 2 * b + 1] = both[rows:].astype(jnp.bfloat16)

        @pl.loop(1, chips)
        def _(i):
            dest = lax.rem(chip + i, chips)
            remote(
                sbuf.at[c, dest], rbuf.at[c, chip], rt_send.at[c], rt_recv.at[c], dest * 2 + core
            ).start()

        rbuf[c, chip] = sbuf[c, chip]

    sub = min(tile, nc)
    for c in range(outs):
        load_d(c).wait()

        @pl.loop(0, nc // sub)
        def _(n):
            cols = pl.ds(pl.multiple_of(n * sub, sub), sub)
            o = jnp.dot(hid[...], down[c, :, cols], preferred_element_type=jnp.float32)
            o = o * share[:, :1]
            mine[c, 0, :, cols] = o[:mates]
            mine[c, 1, :, cols] = o[mates:]

        swap(c).start()
        if c > 0:
            give(c - 1)
    give(outs - 1)

    for c in range(outs):
        many(rbuf.at[c, pl.ds(0, chips - 1)], rt_recv.at[c]).wait()
        total = rbuf[c, 0].astype(jnp.float32)
        if chips <= 16:
            for b in range(1, chips):
                total = total + rbuf[c, b].astype(jnp.float32)
        else:
            total = lax.fori_loop(1, chips, lambda b, t: t + rbuf[c, b].astype(jnp.float32), total)
        out[:, c * nc : (c + 1) * nc] = total.astype(jnp.bfloat16)

    for j in range(units):
        many(rx.at[j, 0, pl.ds(0, chips - 1)], tx_send.at[j]).wait()
        relay(j).wait_send()
    many(ax.at[0, pl.ds(0, chips - 1)], ax_send.at[0]).wait()
    relay_aux.wait_send()
    for c in range(outs):
        swap(c).wait_send()
        many(rbuf.at[c, pl.ds(0, chips - 1)], rt_send.at[c]).wait()


def layer(tokens, routes, gates, wg, wu, wd):
    devices = lax.axis_size("ep")
    rows, width = tokens.shape
    hidden = wg.shape[1]
    chips = devices // 2
    kc, nc = piece(width, 1024), piece(width, 1024)
    tile = piece(hidden, 512)
    units, outs = width // kc, width // nc
    batch = devices * rows
    bf16, f32 = jnp.bfloat16, jnp.float32
    dma = pltpu.SemaphoreType.DMA
    anywhere = pl.BlockSpec(memory_space=pl.ANY)
    vmem = pl.BlockSpec(memory_space=pltpu.VMEM)
    return pl.pallas_call(
        functools.partial(kernel, devices, kc, nc, tile),
        out_shape=jax.ShapeDtypeStruct((rows, width), bf16),
        in_specs=[anywhere, vmem, vmem, anywhere, anywhere, anywhere],
        out_specs=vmem,
        scratch_shapes=[
            pltpu.VMEM((SLOTS, kc, hidden), bf16),
            pltpu.VMEM((SLOTS, kc, hidden), bf16),
            pltpu.VMEM((outs, hidden, nc), bf16),
            pltpu.VMEM((units, 2, chips, rows, kc), bf16),
            pltpu.VMEM((2, chips, rows, AUX), bf16),
            pltpu.VMEM((batch, kc), f32),
            pltpu.VMEM((batch, kc), bf16),
            pltpu.VMEM((batch, hidden), f32),
            pltpu.VMEM((batch, hidden), f32),
            pltpu.VMEM((batch, hidden), bf16),
            pltpu.VMEM((batch, AUX), f32),
            pltpu.VMEM((outs, 2, chips * rows, nc), f32),
            pltpu.VMEM((outs, chips * rows, nc), f32),
            pltpu.VMEM((outs, chips, rows, nc), bf16),
            pltpu.VMEM((outs, chips, rows, nc), bf16),
            dma((units,)), dma((SLOTS,)), dma((SLOTS,)), dma((outs,)),
            dma((units,)), dma((units,)), dma((units,)), dma((units,)),
            dma((outs,)), dma((outs,)), dma((outs,)), dma((outs,)),
            dma((2,)), dma((2,)),
        ],
        compiler_params=pltpu.CompilerParams(
            collective_id=0, has_side_effects=True, vmem_limit_bytes=67_043_328
        ),
    )(tokens, routes, gates, wg, wu, wd)


def solution(mesh):
    placed = (
        P(("groups", "ep"), None),
        P(("groups", "ep"), None),
        P(("groups", "ep"), None),
        P(None, "ep"),
        P(None, "ep"),
        P("ep", None),
    )
    return jax.shard_map(
        layer, mesh=mesh, in_specs=placed, out_specs=P(("groups", "ep"), None), check_vma=False
    )
```

time: 114 us -> 51.6 us (0.45)
  the two profiles are of different devices: /device:TPU:15 before, /device:TPU:0 now
where the time goes in v1:
time: 51.6 us; the launch traced here: 51.4 us
  Pallas kernels  50 us (97%)
  local copies, waits for them, and re-layouts  1.46 us (3%)
    pallas_call x1, Pallas kernels, layer(): pl.pallas_call(functools.partial(kernel, devices, kc, nc, tile), out_shap...  50 us
    unnamed x1, local copies, waits for them, and re-layouts  1.46 us

profile of v1, /device:TPU:0, one launch (start us, length us, event | category | flops | bytes accessed | tf_op | source)
XLA Modules:
  0.0 51.4 jit_solution(16506078574666001110)
XLA Ops:
  0.0 50.0 %shard_map.64 = bf16[4,7168]{1,0:T(4,128)(2,1)} custom-call(bf16[4,7168]{1,0:T(4,128)(2,1)} %tokens.1, s32[4,8]{1,0:T(4,128)} %routes.1, f32[4,8]{1,0:T(4,128)} %gates.1, bf16[7168,2048]{1,0:T(8,128)(2,1)} %wg.1, bf16[7168,2048]{1,0:T(8,128)(2,1)} %wu.1, bf16[2048,7168]{1,0:T(8,128)(2,1)} %wd.1), custom_call_target="tpu_custom_call" | custom-call | tf_op jit(solution)/shard_map/pallas_call | solution.py:249
  50.0 1.5 %copy.8 = bf16[4,7168]{1,0:T(4,128)(2,1)} copy(bf16[4,7168]{1,0:T(4,128)(2,1)} %shard_map.64) | data formatting | bytes 114688

commit v2 on v1

--- a/solution.py
+++ b/solution.py
@@ -63,6 +63,9 @@
     for j in range(min(SLOTS, units)):
         load_g(j).start()
         load_u(j).start()
+    issued = min(2, outs)
+    for c in range(issued):
+        load_d(c).start()
 
     barrier = pltpu.get_barrier_semaphore()
     pl.semaphore_signal(barrier, inc=1, device_id={"ep": peer}, device_id_type=pl.DeviceIdType.MESH)
@@ -110,9 +113,6 @@
         relay(j).start()
 
     forward(0)
-    for c in range(min(1, outs)):
-        load_d(c).start()
-    issued = 1
     for j in range(units):
         if j + 1 < units:
             forward(j + 1)
@@ -133,7 +133,7 @@
         load_u(j).wait()
         s = j % SLOTS
 
-        @pl.loop(0, hidden // tile)
+        @pl.loop(0, hidden // tile, unroll=True)
         def _(n):
             cols = pl.ds(pl.multiple_of(n * tile, tile), tile)
             pg = jnp.dot(xb[...], ring_g[s, :, cols], preferred_element_type=jnp.float32)
@@ -200,7 +200,7 @@
     for c in range(outs):
         load_d(c).wait()
 
-        @pl.loop(0, nc // sub)
+        @pl.loop(0, nc // sub, unroll=True)
         def _(n):
             cols = pl.ds(pl.multiple_of(n * sub, sub), sub)
             o = jnp.dot(hid[...], down[c, :, cols], preferred_element_type=jnp.float32)

time: 51.6 us -> 50.2 us (0.973)
  Pallas kernels: 50 us -> 48.6 us
    pallas_call x1, Pallas kernels: 50 us -> 48.6 us  [layer(): pl.pallas_call(functools.partial(kernel, devices, kc, nc, tile), out_shap...]
where the time goes in v2:
time: 50.2 us; the launch traced here: 50.1 us
  Pallas kernels  48.6 us (97%)
  local copies, waits for them, and re-layouts  1.46 us (3%)
    pallas_call x1, Pallas kernels, layer(): pl.pallas_call(functools.partial(kernel, devices, kc, nc, tile), out_shap...  48.6 us
    unnamed x1, local copies, waits for them, and re-layouts  1.46 us

profile of v2, /device:TPU:0, one launch (start us, length us, event | category | flops | bytes accessed | tf_op | source)
XLA Modules:
  0.0 50.1 jit_solution(13197676122772791115)
XLA Ops:
  0.0 48.6 %shard_map.64 = bf16[4,7168]{1,0:T(4,128)(2,1)} custom-call(bf16[4,7168]{1,0:T(4,128)(2,1)} %tokens.1, s32[4,8]{1,0:T(4,128)} %routes.1, f32[4,8]{1,0:T(4,128)} %gates.1, bf16[7168,2048]{1,0:T(8,128)(2,1)} %wg.1, bf16[7168,2048]{1,0:T(8,128)(2,1)} %wu.1, bf16[2048,7168]{1,0:T(8,128)(2,1)} %wd.1), custom_call_target="tpu_custom_call" | custom-call | tf_op jit(solution)/shard_map/pallas_call | solution.py:249
  48.6 1.5 %copy.8 = bf16[4,7168]{1,0:T(4,128)(2,1)} copy(bf16[4,7168]{1,0:T(4,128)(2,1)} %shard_map.64) | data formatting | bytes 114688
